TPU v7x, 1024 devices: a whole 4x4x32 slice. The times are simulated.
1024 devices in a mesh: dp: 4 (over y), expert: 64 (over z, core), tensor: 4 (over x).
Axes of the slice: x: 4, y: 4, z: 32, core: 2. Of those that a mesh axis runs over, the one named last changes fastest.
Arguments:
- tokens: bfloat16 [1536, 7168], P('expert', 'tensor'), may hold values from -6 to 6
- expert_ids: int32 [1536, 8], P('expert'), may hold values from 0 to 63, all different within a row; in each aligned block of 24 rows (0 to 23, 24 to 47, ...) at most 4 rows name the same one
- gate_weights: float32 [1536, 8], P('expert'), may hold values from 0.1 to 1
- w_gate: bfloat16 [64, 7168, 1024], P('expert', 'tensor', 'dp'), may hold values from -0.0625 to 0.0625
- w_up: bfloat16 [64, 7168, 1024], P('expert', 'tensor', 'dp'), may hold values from -0.0625 to 0.0625
- w_down: bfloat16 [64, 1024, 7168], P('expert', 'dp', 'tensor'), may hold values from -0.1875 to 0.1875
Outputs:
- mixed: bfloat16 [1536, 7168], P('expert', 'tensor')
Inputs may be any that keep to these rules, and one draw needn't show every extreme that they name: `expert_ids`: each row names 8 different experts. Among the rows of one index of the expert axis (aligned blocks of 24 rows) no expert is named more than 4 times, and in some block one expert is named exactly 4 times.
All inputs are finite; a program needn't handle non-finite values.
Results may differ from a plain program's by a relative error of at most 0.0049.
Values may be sent and summed in bfloat16 or wider, within the bound.
A program may use at most 32 MiB of HBM per device.

v0:
```python
import jax
import jax.numpy as jnp
from jax import lax
from jax.sharding import Mesh
from jax.sharding import PartitionSpec as P

TOP = 8
CAP = 4
EXPERT = ("expert_0", "expert_1")


def cut_along(value, dim, size):
    shape = value.shape
    pieces = value.reshape(*shape[:dim], size, shape[dim] // size, *shape[dim + 1 :])
    return jnp.moveaxis(pieces, dim, 0)


def in_order(pieces, dim):
    shape = list(pieces.shape[1:])
    shape[dim] *= pieces.shape[0]
    return jnp.moveaxis(pieces, 0, dim).reshape(shape)


def moved_by_axis(pieces, axes, turns):
    inside = pieces.shape[1:]
    filled = pieces.reshape(*(lax.axis_size(a) for a in axes), *inside)
    for k in turns:
        filled = lax.all_to_all(filled, axes[k], k, k, tiled=True)
    return filled.reshape(-1, *inside)


def two_step_exchange(value, groups, turns, split_dim, concat_dim):
    size = lax.axis_size(groups[0]) * lax.axis_size(groups[1])
    pieces = cut_along(value, split_dim, size)
    return in_order(moved_by_axis(pieces, groups, turns), concat_dim)


def sent_and_summed(value, axis, dim):
    pieces = cut_along(value, dim, lax.axis_size(axis))
    arrived = lax.all_to_all(pieces, axis, split_axis=0, concat_axis=0, tiled=True)
    return arrived.sum(axis=0)


def in_one_piece(arrays, axis, dim, along):
    both = jnp.concatenate(arrays, axis=along)
    filled, at, done = (sent_and_summed(both, axis, dim), 0, [])
    for a in arrays:
        done.append(lax.slice_in_dim(filled, at, at + a.shape[along], axis=along))
        at += a.shape[along]
    return tuple(done)


def sent_to_all(value, axis):
    size = lax.axis_size(axis)
    return lax.all_to_all(
        jnp.broadcast_to(value[None], (size, *value.shape)), axis, 0, 0, tiled=True
    )


def gathered_copies(value, axis, dim):
    return in_order(sent_to_all(value, axis), dim)


def taken_together(value, axis):
    everything = sent_to_all(value, axis)
    return jnp.sum(everything, axis=0)


def per_device(tokens, expert_ids, gate_weights, w_gate, w_up, w_down):
    expert_count = lax.axis_size(EXPERT)
    hidden_count = lax.axis_size("dp")
    local_experts = w_gate.shape[0]
    tok_rows = tokens.shape[0]
    feature_cols = tokens.shape[1]
    total_experts = local_experts * expert_count
    cap_share = CAP // hidden_count
    slot_total = local_experts * CAP * expert_count
    flat_ids = expert_ids.reshape(-1)
    one_hot = (flat_ids[:, None] == lax.iota(jnp.int32, total_experts)[None, :]).astype(jnp.int32)
    earlier = jnp.cumsum(one_hot, axis=0) - one_hot
    slot_rank = jnp.sum(earlier * one_hot, axis=1)
    owner_device = flat_ids // local_experts
    within = flat_ids % local_experts
    send_slot = (within * CAP + slot_rank) * expert_count + owner_device
    dispatch_table = (send_slot[None, :] == lax.iota(jnp.int32, slot_total)[:, None]).astype(
        jnp.float32
    )
    dispatch_table = jnp.sum(dispatch_table.reshape(slot_total, tok_rows, TOP), axis=2).astype(
        jnp.bfloat16
    )
    outbound = jnp.dot(dispatch_table, tokens, preferred_element_type=jnp.float32).astype(
        jnp.bfloat16
    )
    outbound = outbound.reshape(local_experts, CAP, expert_count, feature_cols)
    arrived = two_step_exchange(outbound, ("expert_0", "expert_1"), (1, 0), 2, 2)
    expert_rows = arrived.reshape(local_experts, CAP * expert_count, feature_cols)
    gate_part = jnp.einsum("lrd,ldf->lrf", expert_rows, w_gate, preferred_element_type=jnp.float32)
    up_part = jnp.einsum("lrd,ldf->lrf", expert_rows, w_up, preferred_element_type=jnp.float32)
    gate_sum, up_sum = in_one_piece((gate_part, up_part), "tensor", 1, 0)
    hidden_share = (jax.nn.silu(gate_sum) * up_sum).astype(jnp.bfloat16)
    hidden = gathered_copies(hidden_share, "tensor", 1)
    partial_value = jnp.einsum("lrf,lfd->lrd", hidden, w_down, preferred_element_type=jnp.float32)
    outputs = sent_and_summed(partial_value, "dp", 1)
    backward = outputs.reshape(local_experts, cap_share, expert_count, feature_cols)
    returned = two_step_exchange(backward, ("expert_0", "expert_1"), (1, 0), 2, 2)
    table_cols = local_experts * cap_share * expert_count
    returned = returned.reshape(table_cols, feature_cols)
    block_index = lax.axis_index("dp")
    is_mine = (slot_rank // cap_share == block_index).astype(jnp.float32)
    position = (within * cap_share + slot_rank % cap_share) * expert_count + owner_device
    scaled = gate_weights.reshape(-1) * is_mine
    combine_table = jnp.where(
        position[:, None] == lax.iota(jnp.int32, table_cols)[None, :], scaled[:, None], 0.0
    )
    combine_table = jnp.sum(combine_table.reshape(tok_rows, TOP, table_cols), axis=1)
    partial_mix = jnp.dot(
        combine_table, returned, precision=lax.Precision.HIGHEST, preferred_element_type=jnp.float32
    )
    mixed = taken_together(partial_mix, "dp")
    return mixed.astype(jnp.bfloat16)


def solution(mesh):
    split = Mesh(
        mesh.devices.reshape(mesh.shape["dp"], 32, 2, mesh.shape["tensor"]),
        ("dp", "expert_0", "expert_1", "tensor"),
    )
    placed = (
        P(EXPERT, "tensor"),
        P(EXPERT, None),
        P(EXPERT, None),
        P(EXPERT, "tensor", "dp"),
        P(EXPERT, "tensor", "dp"),
        P(EXPERT, "dp", "tensor"),
    )
    return jax.shard_map(
        per_device, mesh=split, in_specs=placed, out_specs=P(EXPERT, "tensor"), check_vma=False
    )
```

profile of v0, /device:TPU:1, one launch (start us, length us, event | category | flops | bytes accessed | tf_op | source)
XLA Modules:
  0.0 269.3 jit_solution(10628955097788081848)
XLA Ops:
  0.0 0.8 copy.41
  0.8 0.1 eq.69
  1.0 0.6 reduce-window.6
  1.6 0.2 slice_reduce_fusion
  1.8 0.1 bitcast_bitcast_fusion
  2.0 0.1 convert_reduce_fusion
  2.2 1.3 convolution_convert_fusion
  3.5 0.7 copy.47
  4.2 0.2 copy.48
  4.4 18.2 %all_to_all.40 = bf16[32,2,1,4,1,1792]{5,0,3,4,2,1:T(8,128)(2,1)S(1)} all-to-all(bf16[32,2,1,4,1,1792]{5,0,3,4,2,1:T(8,128)(2,1)S(1)} %copy.48), channel_id=1, replica_groups=mesh['dp'=4,'expert_0'=32,'expert_1'=2,'tensor'=4] {'expert_1'}, dimensions={1} | all-to-all | bytes 1835008 | tf_op jit(solution)/shard_map/all_to_all | solution.py:28
  22.6 0.9 copy.49
  23.5 111.6 %all_to_all.41 = bf16[32,2,1,4,1,1792]{5,1,3,4,2,0:T(2,128)(2,1)S(1)} all-to-all(bf16[32,2,1,4,1,1792]{5,1,3,4,2,0:T(2,128)(2,1)S(1)} %copy.49), channel_id=1, replica_groups=mesh['dp'=4,'expert_0'=32,'expert_1'=2,'tensor'=4] {'expert_0'}, dimensions={0} | all-to-all | bytes 1835008 | tf_op jit(solution)/shard_map/all_to_all | solution.py:28
  135.2 0.6 copy.50
  135.8 0.3 reshape.120
  136.2 1.7 convolution_bitcast_fusion.1
  137.9 0.4 convolution_bitcast_fusion.2
  138.4 11.7 %all_to_all.42 = f32[4,2,64,256]{3,2,1,0:T(8,128)S(1)} all-to-all(f32[4,2,64,256]{3,2,1,0:T(8,128)S(1)} %copy.51), channel_id=1, replica_groups=mesh['dp'=4,'expert_0'=32,'expert_1'=2,'tensor'=4] {'tensor'}, dimensions={0} | all-to-all | bytes 1048576 | tf_op jit(solution)/shard_map/all_to_all | solution.py:40
  150.2 7.2 %all_to_all.43 = bf16[4,1,64,256]{3,2,1,0:T(8,128)(2,1)S(1)} all-to-all(bf16[4,1,64,256]{3,2,1,0:T(8,128)(2,1)S(1)} %broadcast_in_dim.21), channel_id=1, replica_groups=mesh['dp'=4,'expert_0'=32,'expert_1'=2,'tensor'=4] {'tensor'}, dimensions={0} | all-to-all | bytes 262144 | tf_op jit(solution)/shard_map/all_to_all | solution.py:55
  157.4 0.4 convolution_bitcast_fusion
  157.8 23.6 %all_to_all.44 = f32[4,1,64,1792]{3,2,1,0:T(8,128)S(1)} all-to-all(f32[4,1,64,1792]{3,2,1,0:T(8,128)S(1)} %convolution_bitcast_fusion), channel_id=1, replica_groups=mesh['dp'=4,'expert_0'=32,'expert_1'=2,'tensor'=4] {'dp'}, dimensions={0} | all-to-all | bytes 3670016 | tf_op jit(solution)/shard_map/all_to_all | solution.py:40
  181.4 0.1 reduce_sum.58
  181.5 0.3 reshape_transpose_reshape_reshape.3
  181.8 8.6 %all_to_all.45 = f32[32,2,1,1,1,1792]{5,0,4,3,2,1:T(8,128)S(1)} all-to-all(f32[32,2,1,1,1,1792]{5,0,4,3,2,1:T(8,128)S(1)} %copy.53), channel_id=1, replica_groups=mesh['dp'=4,'expert_0'=32,'expert_1'=2,'tensor'=4] {'expert_1'}, dimensions={1} | all-to-all | bytes 917504 | tf_op jit(solution)/shard_map/all_to_all | solution.py:28
  190.4 1.1 copy.54
  191.5 6.1 %all-to-all-start.6 = ((f32[32,2,1,1,1,1792]{5,1,4,3,2,0:T(2,128)}), f32[32,2,1,1,1,1792]{5,1,4,3,2,0:T(2,128)S(1)}, u32[]{:S(2)}, u32[]{:S(2)}) async-start(f32[32,2,1,1,1,1792]{5,1,4,3,2,0:T(2,128)} %copy.54), calls=%async_computation.6 | async-start | bytes 917504 | tf_op jit(solution)/shard_map/all_to_all | solution.py:28
  197.7 0.1 eq.78
  197.8 0.1 select_reduce_fusion
  198.0 58.2 %all-to-all-done.6 = f32[32,2,1,1,1,1792]{5,1,4,3,2,0:T(2,128)S(1)} async-done(((f32[32,2,1,1,1,1792]{5,1,4,3,2,0:T(2,128)}), f32[32,2,1,1,1,1792]{5,1,4,3,2,0:T(2,128)S(1)}, u32[]{:S(2)}, u32[]{:S(2)}) %all-to-all-start.6) | async-done | bytes 458784 | tf_op jit(solution)/shard_map/all_to_all | solution.py:28
  256.2 0.3 reshape_reshape_transpose_reshape.3
  256.5 0.3 fusion.11
  256.9 11.7 %all_to_all.46 = f32[4,24,1792]{2,1,0:T(8,128)S(1)} all-to-all(f32[4,24,1792]{2,1,0:T(8,128)S(1)} %broadcast_in_dim.36), channel_id=1, replica_groups=mesh['dp'=4,'expert_0'=32,'expert_1'=2,'tensor'=4] {'dp'}, dimensions={0} | all-to-all | bytes 1376256 | tf_op jit(solution)/shard_map/all_to_all | solution.py:55
  268.6 0.7 reduce_sum.59
  (24 shorter events, 0.5 us)
Async XLA Ops:
  0.0 157.4 %copy-start = (bf16[1,256,1792]{2,1,0:T(8,128)(2,1)S(1)}, bf16[1,256,1792]{2,1,0:T(8,128)(2,1)}, u32[]{:S(2)}) copy-start(bf16[1,256,1792]{2,1,0:T(8,128)(2,1)} %param.11) | copy-start | bytes 2752516
  136.2 1.7 copy-start.1
  181.8 15.8 %copy-start.2 = (f32[24,8]{0,1:T(8,128)S(1)}, f32[24,8]{0,1:T(8,128)}, u32[]{:S(2)}) copy-start(f32[24,8]{0,1:T(8,128)} %param.8) | copy-start | bytes 2308
  191.5 64.6 %all-to-all-start.6 = ((f32[32,2,1,1,1,1792]{5,1,4,3,2,0:T(2,128)}), f32[32,2,1,1,1,1792]{5,1,4,3,2,0:T(2,128)S(1)}, u32[]{:S(2)}, u32[]{:S(2)}) async-start(f32[32,2,1,1,1,1792]{5,1,4,3,2,0:T(2,128)} %copy.54), calls=%async_computation.6 | async-start | bytes 917504 | tf_op jit(solution)/shard_map/all_to_all | solution.py:28
where the time goes:
time: 270 us; the launch traced here: 269 us
  blocking collectives  193 us (71%)
  waiting for transfers between devices  58.2 us (22%)
  starting transfers between devices  6.05 us (2%)
  local copies, waits for them, and re-layouts  5.99 us (2%)
  matrix products  4.14 us (2%)
    all_to_all x3, blocking collectives, moved_by_axis(): filled = lax.all_to_all(filled, axes[k], k, k, tiled=True)  138 us
    all_to_all x1, waiting for transfers between devices, moved_by_axis(): filled = lax.all_to_all(filled, axes[k], k, k, tiled=True)  58.2 us
    all_to_all x2, blocking collectives, sent_and_summed(): lax.all_to_all(pieces, axis, split_axis=0, concat_axis=0, tiled=True)  35.3 us
    all_to_all x2, blocking collectives, sent_to_all(): lax.all_to_all(jnp.broadcast_to(value[None], (size, *value.shape)), axis,...  19 us
    all_to_all x1, starting transfers between devices, moved_by_axis(): filled = lax.all_to_all(filled, axes[k], k, k, tiled=True)  6.05 us
  transfers between devices with their start and end apart: 1, of which 1 were waited for; matrix products, arithmetic and copies ran while one was open for 0% of the time, Pallas kernels for 0%

commit v1 on v0

--- a/solution.py
+++ b/solution.py
@@ -38,7 +38,7 @@
 def sent_and_summed(value, axis, dim):
     pieces = cut_along(value, dim, lax.axis_size(axis))
     arrived = lax.all_to_all(pieces, axis, split_axis=0, concat_axis=0, tiled=True)
-    return arrived.sum(axis=0)
+    return arrived.astype(jnp.float32).sum(axis=0)
 
 
 def in_one_piece(arrays, axis, dim, along):
@@ -74,41 +74,43 @@
     feature_cols = tokens.shape[1]
     total_experts = local_experts * expert_count
     cap_share = CAP // hidden_count
-    slot_total = local_experts * CAP * expert_count
     flat_ids = expert_ids.reshape(-1)
     one_hot = (flat_ids[:, None] == lax.iota(jnp.int32, total_experts)[None, :]).astype(jnp.int32)
     earlier = jnp.cumsum(one_hot, axis=0) - one_hot
     slot_rank = jnp.sum(earlier * one_hot, axis=1)
     owner_device = flat_ids // local_experts
     within = flat_ids % local_experts
-    send_slot = (within * CAP + slot_rank) * expert_count + owner_device
-    dispatch_table = (send_slot[None, :] == lax.iota(jnp.int32, slot_total)[:, None]).astype(
+    block_index = lax.axis_index("dp")
+    is_mine = slot_rank // cap_share == block_index
+    table_cols = local_experts * cap_share * expert_count
+    send_slot = (within * cap_share + slot_rank % cap_share) * expert_count + owner_device
+    mine_at = jnp.where(is_mine, send_slot, -1)
+    dispatch_table = (mine_at[None, :] == lax.iota(jnp.int32, table_cols)[:, None]).astype(
         jnp.float32
     )
-    dispatch_table = jnp.sum(dispatch_table.reshape(slot_total, tok_rows, TOP), axis=2).astype(
+    dispatch_table = jnp.sum(dispatch_table.reshape(table_cols, tok_rows, TOP), axis=2).astype(
         jnp.bfloat16
     )
     outbound = jnp.dot(dispatch_table, tokens, preferred_element_type=jnp.float32).astype(
         jnp.bfloat16
     )
-    outbound = outbound.reshape(local_experts, CAP, expert_count, feature_cols)
+    outbound = outbound.reshape(local_experts, cap_share, expert_count, feature_cols)
     arrived = two_step_exchange(outbound, ("expert_0", "expert_1"), (1, 0), 2, 2)
-    expert_rows = arrived.reshape(local_experts, CAP * expert_count, feature_cols)
+    expert_rows = lax.all_gather(
+        arrived.reshape(local_experts, cap_share * expert_count, feature_cols), "dp", axis=1, tiled=True
+    )
     gate_part = jnp.einsum("lrd,ldf->lrf", expert_rows, w_gate, preferred_element_type=jnp.float32)
     up_part = jnp.einsum("lrd,ldf->lrf", expert_rows, w_up, preferred_element_type=jnp.float32)
     gate_sum, up_sum = in_one_piece((gate_part, up_part), "tensor", 1, 0)
     hidden_share = (jax.nn.silu(gate_sum) * up_sum).astype(jnp.bfloat16)
     hidden = gathered_copies(hidden_share, "tensor", 1)
     partial_value = jnp.einsum("lrf,lfd->lrd", hidden, w_down, preferred_element_type=jnp.float32)
-    outputs = sent_and_summed(partial_value, "dp", 1)
-    backward = outputs.reshape(local_experts, cap_share, expert_count, feature_cols)
+    outputs = sent_and_summed(partial_value.astype(jnp.bfloat16), "dp", 1)
+    backward = outputs.astype(jnp.bfloat16).reshape(local_experts, cap_share, expert_count, feature_cols)
     returned = two_step_exchange(backward, ("expert_0", "expert_1"), (1, 0), 2, 2)
-    table_cols = local_experts * cap_share * expert_count
-    returned = returned.reshape(table_cols, feature_cols)
-    block_index = lax.axis_index("dp")
-    is_mine = (slot_rank // cap_share == block_index).astype(jnp.float32)
-    position = (within * cap_share + slot_rank % cap_share) * expert_count + owner_device
-    scaled = gate_weights.reshape(-1) * is_mine
+    returned = returned.reshape(table_cols, feature_cols).astype(jnp.float32)
+    position = send_slot
+    scaled = gate_weights.reshape(-1) * is_mine.astype(jnp.float32)
     combine_table = jnp.where(
         position[:, None] == lax.iota(jnp.int32, table_cols)[None, :], scaled[:, None], 0.0
     )

time: 270 us -> 192 us (0.71)
  blocking collectives: 193 us -> 139 us
  waiting for transfers between devices: 58.2 us -> 39.4 us
    all_to_all x3, blocking collectives: 138 us -> 84.7 us  [moved_by_axis(): filled = lax.all_to_all(filled, axes[k], k, k, tiled=True)]
    all_to_all x1, waiting for transfers between devices: 58.2 us -> 39.4 us  [moved_by_axis(): filled = lax.all_to_all(filled, axes[k], k, k, tiled=True)]
    all_to_all x2, blocking collectives: 35.3 us -> 22.3 us  [sent_and_summed(): lax.all_to_all(pieces, axis, split_axis=0, concat_axis=0, tiled=True)]
    all_gather x0 -> x1, blocking collectives: none -> 12.8 us  [per_device(): lax.all_gather(arrived.reshape(local_experts, cap_share * expert_count, f...]
where the time goes in v1:
time: 192 us; the launch traced here: 191 us
  blocking collectives  139 us (72%)
  waiting for transfers between devices  39.4 us (21%)
  starting transfers between devices  3.87 us (2%)
  local copies, waits for them, and re-layouts  3.7 us (2%)
  matrix products  2.58 us (1%)
  other arithmetic  2 us (1%)
    all_to_all x3, blocking collectives, moved_by_axis(): filled = lax.all_to_all(filled, axes[k], k, k, tiled=True)  84.7 us
    all_to_all x1, waiting for transfers between devices, moved_by_axis(): filled = lax.all_to_all(filled, axes[k], k, k, tiled=True)  39.4 us
    all_to_all x2, blocking collectives, sent_and_summed(): lax.all_to_all(pieces, axis, split_axis=0, concat_axis=0, tiled=True)  22.3 us
    all_to_all x2, blocking collectives, sent_to_all(): lax.all_to_all(jnp.broadcast_to(value[None], (size, *value.shape)), axis,...  19.7 us
    all_gather x1, blocking collectives, per_device(): lax.all_gather(arrived.reshape(local_experts, cap_share * expert_count, f...  12.8 us
    all_to_all x1, starting transfers between devices, moved_by_axis(): filled = lax.all_to_all(filled, axes[k], k, k, tiled=True)  3.87 us
  transfers between devices with their start and end apart: 1, of which 1 were waited for; matrix products, arithmetic and copies ran while one was open for 0% of the time, Pallas kernels for 0%

profile of v1, /device:TPU:1, one launch (start us, length us, event | category | flops | bytes accessed | tf_op | source)
XLA Modules:
  0.0 191.1 jit_solution(7458012895366178306)
XLA Ops:
  0.0 0.8 copy.39
  0.8 0.1 eq.73
  1.0 0.6 reduce-window.6
  1.6 0.2 slice_reduce_fusion
  1.8 0.1 bitcast_bitcast_fusion
  2.0 0.1 eq.82
  2.1 0.1 convert_reduce_fusion
  2.2 1.1 convolution_convert_fusion.1
  3.3 0.1 reshape_transpose_reshape_reshape.6
  3.5 17.7 %all_to_all.40 = bf16[32,2,1,1,1,1792]{5,0,4,3,2,1:T(8,128)(2,1)S(1)} all-to-all(bf16[32,2,1,1,1,1792]{5,0,4,3,2,1:T(8,128)(2,1)S(1)} %copy.45), channel_id=1, replica_groups=mesh['dp'=4,'expert_0'=32,'expert_1'=2,'tensor'=4] {'expert_1'}, dimensions={1} | all-to-all | bytes 458752 | tf_op jit(solution)/shard_map/all_to_all | solution.py:28
  21.1 0.2 copy.46
  21.3 54.7 %all_to_all.41 = bf16[32,2,1,1,1,1792]{5,1,4,3,2,0:T(2,128)(2,1)S(1)} all-to-all(bf16[32,2,1,1,1,1792]{5,1,4,3,2,0:T(2,128)(2,1)S(1)} %copy.46), channel_id=1, replica_groups=mesh['dp'=4,'expert_0'=32,'expert_1'=2,'tensor'=4] {'expert_0'}, dimensions={0} | all-to-all | bytes 458752 | tf_op jit(solution)/shard_map/all_to_all | solution.py:28
  76.1 0.1 reshape_reshape_transpose_reshape.6
  76.2 12.8 %all_gather.3 = bf16[1,256,1792]{2,1,0:T(8,128)(2,1)S(1)} all-gather(bf16[1,64,1792]{2,1,0:T(8,128)(2,1)S(1)} %reshape_reshape_transpose_reshape.6), channel_id=1, replica_groups=mesh['dp'=4,'expert_0'=32,'expert_1'=2,'tensor'=4] {'dp'}, dimensions={1}, use_global_device_ids=true | all-gather | bytes 1146880 | tf_op jit(solution)/shard_map/all_gather | solution.py:99
  89.0 0.4 convolution_bitcast_fusion
  89.4 0.8 copy-done.2
  90.1 0.4 convolution_bitcast_fusion.1
  90.6 10.7 %all_to_all.42 = f32[4,2,64,256]{3,2,1,0:T(8,128)S(1)} all-to-all(f32[4,2,64,256]{3,2,1,0:T(8,128)S(1)} %copy.47), channel_id=1, replica_groups=mesh['dp'=4,'expert_0'=32,'expert_1'=2,'tensor'=4] {'tensor'}, dimensions={0} | all-to-all | bytes 1048576 | tf_op jit(solution)/shard_map/all_to_all | solution.py:40
  101.5 7.2 %all_to_all.43 = bf16[4,1,64,256]{3,2,1,0:T(8,128)(2,1)S(1)} all-to-all(bf16[4,1,64,256]{3,2,1,0:T(8,128)(2,1)S(1)} %broadcast_in_dim.23), channel_id=1, replica_groups=mesh['dp'=4,'expert_0'=32,'expert_1'=2,'tensor'=4] {'tensor'}, dimensions={0} | all-to-all | bytes 262144 | tf_op jit(solution)/shard_map/all_to_all | solution.py:55
  108.7 0.4 convolution_convert_fusion
  109.1 11.5 %all_to_all.44 = bf16[4,1,64,1792]{3,2,1,0:T(8,128)(2,1)S(1)} all-to-all(bf16[4,1,64,1792]{3,2,1,0:T(8,128)(2,1)S(1)} %bitcast.49), channel_id=1, replica_groups=mesh['dp'=4,'expert_0'=32,'expert_1'=2,'tensor'=4] {'dp'}, dimensions={0} | all-to-all | bytes 1835008 | tf_op jit(solution)/shard_map/all_to_all | solution.py:40
  120.7 0.2 reduce_sum.61
  120.8 0.1 reshape_transpose_reshape_reshape.7
  121.0 12.3 %all_to_all.45 = bf16[32,2,1,1,1,1792]{5,0,4,3,2,1:T(8,128)(2,1)S(1)} all-to-all(bf16[32,2,1,1,1,1792]{5,0,4,3,2,1:T(8,128)(2,1)S(1)} %copy.49), channel_id=1, replica_groups=mesh['dp'=4,'expert_0'=32,'expert_1'=2,'tensor'=4] {'expert_1'}, dimensions={1} | all-to-all | bytes 458752 | tf_op jit(solution)/shard_map/all_to_all | solution.py:28
  133.2 0.9 copy.50
  134.1 3.9 %all-to-all-start.6 = ((bf16[32,2,1,1,1,1792]{5,1,4,3,2,0:T(2,128)(2,1)}), bf16[32,2,1,1,1,1792]{5,1,4,3,2,0:T(2,128)(2,1)S(1)}, u32[]{:S(2)}, u32[]{:S(2)}) async-start(bf16[32,2,1,1,1,1792]{5,1,4,3,2,0:T(2,128)(2,1)} %copy.50), calls=%async_computation.6 | async-start | bytes 458752 | tf_op jit(solution)/shard_map/all_to_all | solution.py:28
  138.1 0.1 select_reduce_fusion
  138.2 39.4 %all-to-all-done.6 = bf16[32,2,1,1,1,1792]{5,1,4,3,2,0:T(2,128)(2,1)S(1)} async-done(((bf16[32,2,1,1,1,1792]{5,1,4,3,2,0:T(2,128)(2,1)}), bf16[32,2,1,1,1,1792]{5,1,4,3,2,0:T(2,128)(2,1)S(1)}, u32[]{:S(2)}, u32[]{:S(2)}) %all-to-all-start.6) | async-done | bytes 229408 | tf_op jit(solution)/shard_map/all_to_all | solution.py:28
  177.6 0.1 reshape_reshape_transpose_reshape.7
  177.7 0.2 fusion.8
  178.0 12.5 %all_to_all.46 = f32[4,24,1792]{2,1,0:T(8,128)S(1)} all-to-all(f32[4,24,1792]{2,1,0:T(8,128)S(1)} %broadcast_in_dim.38), channel_id=1, replica_groups=mesh['dp'=4,'expert_0'=32,'expert_1'=2,'tensor'=4] {'dp'}, dimensions={0} | all-to-all | bytes 1376256 | tf_op jit(solution)/shard_map/all_to_all | solution.py:55
  190.5 0.7 reduce_sum.62
  (24 shorter events, 0.5 us)
Async XLA Ops:
  0.0 108.7 %copy-start = (bf16[1,256,1792]{2,1,0:T(8,128)(2,1)S(1)}, bf16[1,256,1792]{2,1,0:T(8,128)(2,1)}, u32[]{:S(2)}) copy-start(bf16[1,256,1792]{2,1,0:T(8,128)(2,1)} %param.11) | copy-start | bytes 2752516
  76.1 12.9 %copy-start.1 = (bf16[1,1792,256]{2,1,0:T(8,128)(2,1)S(1)}, bf16[1,1792,256]{2,1,0:T(8,128)(2,1)}, u32[]{:S(2)}) copy-start(bf16[1,1792,256]{2,1,0:T(8,128)(2,1)} %param.10) | copy-start | bytes 2752516
  89.0 1.2 copy-start.2
  120.9 17.1 %copy-start.3 = (f32[24,8]{0,1:T(8,128)S(1)}, f32[24,8]{0,1:T(8,128)}, u32[]{:S(2)}) copy-start(f32[24,8]{0,1:T(8,128)} %param.8) | copy-start | bytes 2308
  134.1 43.5 %all-to-all-start.6 = ((bf16[32,2,1,1,1,1792]{5,1,4,3,2,0:T(2,128)(2,1)}), bf16[32,2,1,1,1,1792]{5,1,4,3,2,0:T(2,128)(2,1)S(1)}, u32[]{:S(2)}, u32[]{:S(2)}) async-start(bf16[32,2,1,1,1,1792]{5,1,4,3,2,0:T(2,128)(2,1)} %copy.50), calls=%async_computation.6 | async-start | bytes 458752 | tf_op jit(solution)/shard_map/all_to_all | solution.py:28

commit v2 on v0

v2 whole, which is shorter than its diff:
```python
import jax
import jax.numpy as jnp
from jax import lax
from jax.experimental import pallas as pl
from jax.experimental.pallas import tpu as pltpu
from jax.sharding import PartitionSpec as P

TOP = 8
CAP = 4
NZ = 32
NX = 4
NY = 4
TOK = 24
PADTOK = 32
LANES = 512
EDGE = 64
WINDOW = 4
CHUNKS = 4
HALF = WINDOW * 2 * CAP
ROWS = 2 * HALF
SHARE = ROWS // NX
BASES = (0, 384, 896, 1280)
F32 = jnp.float32
BF16 = jnp.bfloat16


def spread_tree():
    parent = {}
    for o in (4, 8, 12, 16):
        parent[o] = o - 4
    for o in (-4, -8, -12):
        parent[o] = o + 4
    for o in (0, 4, 8, 12):
        parent[o + 1] = o
        parent[o + 2] = o + 1
    for o in (4, 8, 12, 16):
        parent[o - 1] = o
    for o in (0, -4, -8, -12):
        parent[o - 1] = o
        parent[o - 2] = o - 1
    for o in (-4, -8, -12):
        parent[o + 1] = o
    parent[-15] = -14
    return parent


PARENT = spread_tree()
HOP = (1.7, 0.8)
STEP = {"over": 1.5, "gather": 5.0, "sum": 4.5, "hidden": 2.6, "down": 5.0, "back": 18.0}


def plan():
    arrival = {0: 0.0}
    while len(arrival) < NZ:
        for o, p in PARENT.items():
            if o not in arrival and p in arrival:
                arrival[o] = arrival[p] + HOP[0] + HOP[1] * abs(o - p)
    order = sorted(arrival, key=lambda o: (arrival[o], o))
    children = {o: sorted([c for c in PARENT if PARENT[c] == o], key=lambda c: -abs(c - o)) for o in order}
    return arrival, order, children


ARRIVAL, ORDER, CHILDREN = plan()
REACH = sorted({(c - p) % NZ for c, p in PARENT.items()} | {(p - c) % NZ for c, p in PARENT.items()})


def groups_of(i):
    return (i, NZ // WINDOW - 1 - i)


def offsets_of(i):
    return [g * WINDOW + j for g in groups_of(i) for j in range(WINDOW)]


def body(tok_ref, ids_ref, gates_ref, wg_ref, wu_ref, wd_ref, out_ref,
         wg, wu, wd, tv, idv, gav, ga, gb, rows, gu, xin, hid, down, yin, ret, back, table, acc, part, fin,
         lsem, msem, mrem, asem, arem, bsem, brem, ysem, yrem, xsem, xrem, hsem, hrem, dsem, drem, zsem, zrem, psem, fsem, frem):
    e = lax.axis_index("expert")
    x = lax.axis_index("tensor")
    y = lax.axis_index("dp")
    z = e // 2
    c = e % 2
    odd = y % 2
    partner = {"expert": 2 * z + (1 - c)}

    def at_z(off):
        return {"expert": 2 * lax.rem(z + (off % NZ), NZ) + c}

    def at_x(d):
        return {"tensor": lax.rem(x + d, NX)}

    def at_y(d):
        return {"dp": lax.rem(y + d, NY)}

    sent = []

    def remote(src, dst, s, r, to):
        return pltpu.make_async_remote_copy(src_ref=src, dst_ref=dst, send_sem=s, recv_sem=r, device_id=to)

    def send(copy):
        copy.start()
        sent.append(copy)

    pad = jnp.zeros((NZ, PADTOK - TOK, LANES), BF16)
    ga[:, TOK:, :] = pad
    gb[:, TOK:, :] = pad
    barrier = pltpu.get_barrier_semaphore()
    pl.semaphore_signal(barrier, inc=1, device_id=partner)
    for off in REACH:
        pl.semaphore_signal(barrier, inc=1, device_id=at_z(off))
    for d in range(1, NX):
        pl.semaphore_signal(barrier, inc=1, device_id=at_x(d))
    for d in range(1, NY):
        pl.semaphore_signal(barrier, inc=1, device_id=at_y(d))
    base = pl.multiple_of(((7 * y) // 2) * 128, 128)
    loads = [
        pltpu.make_async_copy(tok_ref.at[:, pl.ds(base, LANES)], tv, lsem.at[0]),
        pltpu.make_async_copy(ids_ref, idv.at[0], lsem.at[1]),
        pltpu.make_async_copy(gates_ref, gav.at[0], lsem.at[2]),
        pltpu.make_async_copy(wg_ref, wg, lsem.at[3]),
        pltpu.make_async_copy(wu_ref, wu, lsem.at[4]),
        pltpu.make_async_copy(wd_ref, wd, lsem.at[5]),
    ]
    for copy in loads:
        copy.start()

    def own_lanes(shape):
        lane = lax.broadcasted_iota(jnp.int32, shape, len(shape) - 1)
        return jnp.logical_and(lane >= EDGE * odd, lane < LANES - EDGE + EDGE * odd)

    first_id = (LANES - EDGE) * (1 - odd)
    for copy in loads[:3]:
        copy.wait()
    spot = lax.broadcasted_iota(jnp.int32, (TOP, LANES), 1) == first_id + lax.broadcasted_iota(jnp.int32, (TOP, LANES), 0)
    ids_wide = jnp.dot(idv[0].astype(F32), jnp.where(spot, 1.0, 0.0), precision=lax.Precision.HIGHEST, preferred_element_type=F32)
    ga[0, :TOK, :] = jnp.where(own_lanes((TOK, LANES)), tv[...].astype(F32), ids_wide).astype(BF16)
    pl.semaphore_wait(barrier, 1 + len(REACH) + NX - 1 + NY - 1)

    def block(ref, k):
        return ref.at[k, pl.ds(0, TOK), :]

    def relay(child):
        k = (-PARENT[child]) % NZ
        j = (-child) % NZ
        return remote(block(ga, k), block(ga, j), asem.at[j], arem.at[j], at_z(child - PARENT[child]))

    def over(k):
        return remote(block(ga, k), block(gb, k), bsem.at[k], brem.at[k], partner)

    metas = [
        remote(idv.at[0], idv.at[1], msem.at[0], mrem.at[0], partner),
        remote(gav.at[0], gav.at[1], msem.at[1], mrem.at[1], partner),
    ]

    def pass_on(o):
        k = (-o) % NZ
        if o != 0:
            relay(o).wait_recv()
        for child in CHILDREN[o]:
            send(relay(child))
        send(over(k))
        if o == 0:
            for copy in metas:
                send(copy)

    def make_table():
        for copy in metas:
            copy.wait_recv()
        col = lax.broadcasted_iota(jnp.int32, (2 * TOK, ROWS), 1)
        row = lax.broadcasted_iota(jnp.int32, (2 * TOK, ROWS), 0)
        ids = jnp.concatenate([idv[0], idv[1]], axis=0)
        gates = jnp.concatenate([gav[0], gav[1]], axis=0)
        tri_i = lax.broadcasted_iota(jnp.int32, (2 * TOK, 2 * TOK), 0)
        tri_j = lax.broadcasted_iota(jnp.int32, (2 * TOK, 2 * TOK), 1)
        tri = jnp.where(jnp.logical_and(tri_j < tri_i, tri_i // TOK == tri_j // TOK), 1.0, 0.0).astype(BF16)
        slot = (col % (2 * CAP) - CAP * (row // TOK)).astype(F32)
        for i in range(CHUNKS):
            lo, hi = groups_of(i)
            dz = jnp.where(col < HALF, lo * WINDOW, hi * WINDOW) + (col % HALF) // (2 * CAP)
            wanted = 2 * lax.rem(z + NZ - dz, NZ) + c
            hits = jnp.zeros((2 * TOK, ROWS), F32)
            share = jnp.zeros((2 * TOK, ROWS), F32)
            for k in range(TOP):
                same = ids[:, k:k + 1] == wanted
                hits = hits + jnp.where(same, 1.0, 0.0)
                share = share + jnp.where(same, gates[:, k:k + 1], 0.0)
            rank = jnp.dot(tri, hits.astype(BF16), preferred_element_type=F32)
            table[i] = jnp.where(rank == slot, share, 0.0)

    tok = WINDOW * PADTOK
    lane = lax.broadcasted_iota(jnp.int32, (tok, 128), 1) - EDGE * (1 - odd)
    id_lane = jnp.logical_and(lane >= 0, lane < TOP)
    before_i = lax.broadcasted_iota(jnp.int32, (tok, tok), 0)
    before_j = lax.broadcasted_iota(jnp.int32, (tok, tok), 1)
    before = jnp.where(
        jnp.logical_and(before_i < before_j, before_i // PADTOK == before_j // PADTOK), 1.0, 0.0
    ).astype(BF16)
    slot_of = lax.broadcasted_iota(jnp.int32, (HALF, tok), 0)
    tok_of = lax.broadcasted_iota(jnp.int32, (HALF, tok), 1)
    ones = jnp.ones((HALF, 128), BF16)

    def chosen(held, p):
        ids = jnp.where(odd == 1, held[:, :128].astype(F32), held[:, LANES - 128:].astype(F32))
        named = jnp.where(jnp.logical_and(id_lane, ids == e.astype(F32)), 1.0, 0.0).astype(BF16)
        hit = lax.dot_general(ones, named, (((1,), (1,)), ((), ())), preferred_element_type=F32)
        rank = jnp.dot(hit.astype(BF16), before, preferred_element_type=F32)
        at = ((tok_of // PADTOK) * (2 * CAP) + p * CAP).astype(F32)
        pick = jnp.where(rank + at == slot_of.astype(F32), hit, 0.0).astype(BF16)
        return jnp.dot(pick, held, preferred_element_type=F32)

    def row_copy(i, d):
        return remote(rows.at[y, i], rows.at[y, i], ysem.at[i, d], yrem.at[i, d], at_y(d))

    def select(i):
        for k in offsets_of(i):
            over(k).wait_recv()
        for n, g in enumerate(groups_of(i)):
            own = ga[g * WINDOW:(g + 1) * WINDOW].reshape(tok, LANES)
            other = gb[g * WINDOW:(g + 1) * WINDOW].reshape(tok, LANES)
            picked = chosen(own, 0) + chosen(other, 1)
            rows[y, i, n * HALF:(n + 1) * HALF, :] = jnp.where(own_lanes((HALF, LANES)), picked, 0.0).astype(BF16)
        for d in (2, 1, 3):
            send(row_copy(i, d))

    def sum_copy(i, d):
        return remote(gu.at[i, lax.rem(x + d, NX)], xin.at[i, d - 1], xsem.at[i, d], xrem.at[i, d], at_x(d))

    def multiply(i):
        if i == 0:
            loads[3].wait()
            loads[4].wait()
        for d in (1, 3, 2):
            row_copy(i, d).wait_recv()
        for n, w in ((0, wg), (1, wu)):
            total = jnp.dot(rows[0, i], w[:LANES, :], preferred_element_type=F32)
            for q in range(1, NY):
                total = total + jnp.dot(rows[q, i], w[BASES[q]:BASES[q] + LANES, :], preferred_element_type=F32)
            gu[i, :, :, n * 256:(n + 1) * 256] = total.reshape(NX, SHARE, 256)
        for d in (2, 1, 3):
            send(sum_copy(i, d))

    def hid_copy(i, d):
        return remote(hid.at[i, x], hid.at[i, x], hsem.at[i, d], hrem.at[i, d], at_x(d))

    def activate(i):
        for d in (1, 3, 2):
            sum_copy(i, d).wait_recv()
        sums = (gu[i, x] + xin[i, 0]) + (xin[i, 1] + xin[i, 2])
        gate = sums[:, :256]
        up = sums[:, 256:]
        hid[i, x] = (gate / (1.0 + jnp.exp(-gate)) * up).astype(BF16)
        for d in (2, 1, 3):
            send(hid_copy(i, d))

    def down_copy(i, d):
        return remote(down.at[i, lax.rem(y + d, NY)], yin.at[i, d - 1], dsem.at[i, d], drem.at[i, d], at_y(d))

    def project(i):
        if i == 0:
            loads[5].wait()
        for d in (1, 3, 2):
            hid_copy(i, d).wait_recv()
        hidden = hid[i].reshape(ROWS, 256)
        for q in range(NY):
            down[i, q] = jnp.dot(hidden, wd[:, BASES[q]:BASES[q] + LANES], preferred_element_type=F32).astype(BF16)
        for d in (2, 1, 3):
            send(down_copy(i, d))

    def back_copy(k):
        return remote(ret.at[k], back.at[k], zsem.at[k], zrem.at[k], at_z(k))

    def give_back(i):
        for d in (1, 3, 2):
            down_copy(i, d).wait_recv()
        result = (down[i, y].astype(F32) + yin[i, 0].astype(F32)) + (yin[i, 1].astype(F32) + yin[i, 2].astype(F32))
        result = result.reshape(2, WINDOW, 2 * CAP, LANES).astype(BF16)
        for n, g in enumerate(groups_of(i)):
            ret[g * WINDOW:(g + 1) * WINDOW] = result[n]
        for k in sorted(offsets_of(i), key=lambda k: -min(k, NZ - k)):
            if k == 0:
                back[0] = ret[0]
            else:
                send(back_copy(k))

    def mix(i):
        for k in offsets_of(i):
            if k != 0:
                back_copy(k).wait_recv()
        arrived = jnp.concatenate(
            [back[g * WINDOW:(g + 1) * WINDOW].astype(F32).reshape(HALF, LANES) for g in groups_of(i)], axis=0
        )
        mixed = jnp.dot(table[i], arrived, precision=lax.Precision.HIGHEST, preferred_element_type=F32)
        acc[...] = mixed if i == 0 else acc[...] + mixed

    events = [(ARRIVAL[o], n, pass_on, o) for n, o in enumerate(ORDER)]
    events.append((0.1, 99, lambda _: make_table(), 0))
    for i in range(CHUNKS):
        at = max(ARRIVAL[o] for o in ARRIVAL if (-o) % NZ in offsets_of(i)) + STEP["over"]
        for n, (stage, wait) in enumerate((
            (select, "gather"), (multiply, "sum"), (activate, "hidden"), (project, "down"), (give_back, "back"), (mix, "over"),
        )):
            events.append((at, 100 - n, stage, i))
            at += STEP[wait]
    for _, _, stage, i in sorted(events, key=lambda v: v[:2] + (v[3],)):
        stage(i)

    part[0] = acc[TOK:, :]
    part_copy = remote(part.at[0], part.at[1], psem.at[0], psem.at[1], partner)
    send(part_copy)
    part_copy.wait_recv()
    fin[y] = (acc[:TOK, :] + part[1]).astype(BF16)

    def fin_copy(d):
        return remote(fin.at[y], fin.at[y], fsem.at[d], frem.at[d], at_y(d))

    for d in (2, 1, 3):
        send(fin_copy(d))
    for d in (1, 3, 2):
        fin_copy(d).wait_recv()
    left = lax.broadcasted_iota(jnp.int32, (TOK, 128), 1) < EDGE
    for n in range(2):
        a, b, o = fin[2 * n], fin[2 * n + 1], n * 896
        out_ref[:, o:o + 384] = a[:, :384]
        out_ref[:, o + 384:o + 512] = jnp.where(left, a[:, 384:].astype(F32), b[:, :128].astype(F32)).astype(BF16)
        out_ref[:, o + 512:o + 896] = b[:, 128:]
    for copy in sent:
        copy.wait_send()


def per_device(tokens, expert_ids, gate_weights, w_gate, w_up, w_down):
    dma = pltpu.SemaphoreType.DMA
    vm = pltpu.VMEM
    out = pl.pallas_call(
        body,
        out_shape=jax.ShapeDtypeStruct((TOK, 1792), BF16),
        in_specs=[pl.BlockSpec(memory_space=pl.ANY)] * 6,
        out_specs=pl.BlockSpec(memory_space=pltpu.VMEM),
        scratch_shapes=[
            vm((1792, 256), BF16),
            vm((1792, 256), BF16),
            vm((256, 1792), BF16),
            vm((TOK, LANES), BF16),
            vm((2, TOK, TOP), jnp.int32),
            vm((2, TOK, TOP), F32),
            vm((NZ, PADTOK, LANES), BF16),
            vm((NZ, PADTOK, LANES), BF16),
            vm((NY, CHUNKS, ROWS, LANES), BF16),
            vm((CHUNKS, NX, SHARE, 512), F32),
            vm((CHUNKS, NX - 1, SHARE, 512), F32),
            vm((CHUNKS, NX, SHARE, 256), BF16),
            vm((CHUNKS, NY, ROWS, LANES), BF16),
            vm((CHUNKS, NY - 1, ROWS, LANES), BF16),
            vm((NZ, 2 * CAP, LANES), BF16),
            vm((NZ, 2 * CAP, LANES), BF16),
            vm((CHUNKS, 2 * TOK, ROWS), F32),
            vm((2 * TOK, LANES), F32),
            vm((2, TOK, LANES), F32),
            vm((NY, TOK, LANES), BF16),
            dma((6,)), dma((2,)), dma((2,)),
            dma((NZ,)), dma((NZ,)), dma((NZ,)), dma((NZ,)),
            *[dma((CHUNKS, 4))] * 8,
            dma((NZ,)), dma((NZ,)), dma((2,)), dma((4,)), dma((4,)),
        ],
        compiler_params=pltpu.CompilerParams(
            collective_id=0, has_side_effects=True, vmem_limit_bytes=60 * 1024 * 1024
        ),
    )(tokens, expert_ids, gate_weights, w_gate.reshape(1792, 256), w_up.reshape(1792, 256), w_down.reshape(256, 1792))
    return out


def solution(mesh):
    placed = (
        P("expert", "tensor"),
        P("expert", None),
        P("expert", None),
        P("expert", "tensor", "dp"),
        P("expert", "tensor", "dp"),
        P("expert", "dp", "tensor"),
    )
    return jax.shard_map(
        per_device, mesh=mesh, in_specs=placed, out_specs=P("expert", "tensor"), check_vma=False
    )
```

time: 270 us -> 103 us (0.38)
  blocking collectives: 193 us -> 0 us
  Pallas kernels: 0 us -> 99.2 us
  waiting for transfers between devices: 58.2 us -> 0 us
  starting transfers between devices: 6.05 us -> 0 us
  matrix products: 4.14 us -> 0 us
    all_to_all x7 -> x0, blocking collectives: 193 us -> none  [the longest x3 138 us: moved_by_axis(): filled = lax.all_to_all(filled, axes[k], k, k, tiled=True)]
    pallas_call x0 -> x1, Pallas kernels: none -> 99.2 us  [per_device(): pl.pallas_call(body, out_shape=jax.ShapeDtypeStruct((TOK, 1792), BF16), i...]
    all_to_all x1 -> x0, waiting for transfers between devices: 58.2 us -> none  [moved_by_axis(): filled = lax.all_to_all(filled, axes[k], k, k, tiled=True)]
    all_to_all x1 -> x0, starting transfers between devices: 6.05 us -> none  [moved_by_axis(): filled = lax.all_to_all(filled, axes[k], k, k, tiled=True)]
    dot_general x5 -> x0, matrix products: 4.14 us -> none  [the longest x1 1.67 us: per_device(): jnp.einsum('lrd,ldf->lrf', expert_rows, w_up, preferred_element_type=jnp....]
    all_to_all x3 -> x0, local copies, waits for them, and re-layouts: 2.7 us -> none  [moved_by_axis(): filled = lax.all_to_all(filled, axes[k], k, k, tiled=True)]
  transfers between devices with their start and end apart: 1 -> 0, of which waited for: 1 -> 0; matrix products, arithmetic and copies ran while one was open for 0% -> 0% of each run, Pallas kernels for 0% -> 0%
where the time goes in v2:
time: 103 us
  Pallas kernels  99.2 us (96%)
  local copies, waits for them, and re-layouts  3.57 us (3%)
    pallas_call x1, Pallas kernels, per_device(): pl.pallas_call(body, out_shape=jax.ShapeDtypeStruct((TOK, 1792), BF16), i...  99.2 us
    unnamed x7, local copies, waits for them, and re-layouts  3.57 us

profile of v2, /device:TPU:1, one launch (start us, length us, event | category | flops | bytes accessed | tf_op | source)
XLA Modules:
  0.0 102.7 jit_solution(13882475718749424111)
XLA Ops:
  0.0 0.0 copy-start
  0.0 0.7 copy-done
  0.7 0.0 copy-start.1
  0.7 0.7 copy.7.ids_ref
  1.4 0.0 copy-done.1
  1.4 0.7 copy.8.gates_ref
  2.0 99.2 %shard_map.64 = bf16[24,1792]{1,0:T(8,128)(2,1)} custom-call(bf16[24,1792]{1,0:T(8,128)(2,1)} %tok_ref.1, s32[24,8]{1,0:T(8,128)} %copy.7.ids_ref, f32[24,8]{1,0:T(8,128)} %copy.8.gates_ref, bf16[1792,256]{1,0:T(8,128)(2,1)} %bitcast.3, bf16[1792,256]{1,0:T(8,128)(2,1)} %bitcast.4, bf16[256,1792]{1,0:T(8,128)(2,1)} %bitcast.5), custom_call_target="tpu_custom_call" | custom-call | tf_op jit(solution)/shard_map/pallas_call | solution.py:333
  101.2 1.5 %copy.10 = bf16[24,1792]{1,0:T(8,128)(2,1)} copy(bf16[24,1792]{1,0:T(8,128)(2,1)} %shard_map.64) | data formatting | bytes 172032
Async XLA Ops:
  0.0 0.7 copy-start
  0.7 0.7 copy-start.1

commit v3 on v2

--- a/solution.py
+++ b/solution.py
@@ -14,8 +14,8 @@
 PADTOK = 32
 LANES = 512
 EDGE = 64
-WINDOW = 4
-CHUNKS = 4
+WINDOW = 2
+CHUNKS = 8
 HALF = WINDOW * 2 * CAP
 ROWS = 2 * HALF
 SHARE = ROWS // NX
@@ -45,8 +45,8 @@
 
 
 PARENT = spread_tree()
-HOP = (1.7, 0.8)
-STEP = {"over": 1.5, "gather": 5.0, "sum": 4.5, "hidden": 2.6, "down": 5.0, "back": 18.0}
+HOP = (2.0, 0.7)
+STEP = {"over": 2.5, "gather": 5.2, "sum": 4.8, "hidden": 3.2, "down": 5.2, "back": 18.0}
 
 
 def plan():
@@ -72,9 +72,13 @@
     return [g * WINDOW + j for g in groups_of(i) for j in range(WINDOW)]
 
 
+def chunk_of(k):
+    return next(i for i in range(CHUNKS) if k in offsets_of(i))
+
+
 def body(tok_ref, ids_ref, gates_ref, wg_ref, wu_ref, wd_ref, out_ref,
-         wg, wu, wd, tv, idv, gav, ga, gb, rows, gu, xin, hid, down, yin, ret, back, table, acc, part, fin,
-         lsem, msem, mrem, asem, arem, bsem, brem, ysem, yrem, xsem, xrem, hsem, hrem, dsem, drem, zsem, zrem, psem, fsem, frem):
+         wg, wu, wd, tv, idv, gav, ga, gb, rows, gu, xin, hid, down, yin, ret, back, table, acc, part, fin, outv,
+         lsem, msem, mrem, ssem, arem, brem, yrem, xrem, hrem, drem, zrem, psem, frem):
     e = lax.axis_index("expert")
     x = lax.axis_index("tensor")
     y = lax.axis_index("dp")
@@ -92,14 +96,19 @@
     def at_y(d):
         return {"dp": lax.rem(y + d, NY)}
 
-    sent = []
+    def turned(a, b):
+        return lax.dot_general(
+            a, b, (((0,), (0,)), ((), ())), precision=lax.Precision.HIGHEST, preferred_element_type=F32
+        )
 
     def remote(src, dst, s, r, to):
         return pltpu.make_async_remote_copy(src_ref=src, dst_ref=dst, send_sem=s, recv_sem=r, device_id=to)
 
     def send(copy):
         copy.start()
-        sent.append(copy)
+
+    def all_of(ref, sem):
+        pltpu.make_async_copy(ref, ref, sem).wait()
 
     pad = jnp.zeros((NZ, PADTOK - TOK, LANES), BF16)
     ga[:, TOK:, :] = pad
@@ -132,7 +141,7 @@
     for copy in loads[:3]:
         copy.wait()
     spot = lax.broadcasted_iota(jnp.int32, (TOP, LANES), 1) == first_id + lax.broadcasted_iota(jnp.int32, (TOP, LANES), 0)
-    ids_wide = jnp.dot(idv[0].astype(F32), jnp.where(spot, 1.0, 0.0), precision=lax.Precision.HIGHEST, preferred_element_type=F32)
+    ids_wide = turned(idv[0].astype(F32), jnp.where(spot, 1.0, 0.0))
     ga[0, :TOK, :] = jnp.where(own_lanes((TOK, LANES)), tv[...].astype(F32), ids_wide).astype(BF16)
     pl.semaphore_wait(barrier, 1 + len(REACH) + NX - 1 + NY - 1)
 
@@ -142,10 +151,10 @@
     def relay(child):
         k = (-PARENT[child]) % NZ
         j = (-child) % NZ
-        return remote(block(ga, k), block(ga, j), asem.at[j], arem.at[j], at_z(child - PARENT[child]))
+        return remote(block(ga, k), block(ga, j), ssem.at[0], arem.at[j], at_z(child - PARENT[child]))
 
     def over(k):
-        return remote(block(ga, k), block(gb, k), bsem.at[k], brem.at[k], partner)
+        return remote(block(ga, k), block(gb, k), ssem.at[1], brem.at[chunk_of(k)], partner)
 
     metas = [
         remote(idv.at[0], idv.at[1], msem.at[0], mrem.at[0], partner),
@@ -168,8 +177,9 @@
             copy.wait_recv()
         col = lax.broadcasted_iota(jnp.int32, (2 * TOK, ROWS), 1)
         row = lax.broadcasted_iota(jnp.int32, (2 * TOK, ROWS), 0)
-        ids = jnp.concatenate([idv[0], idv[1]], axis=0)
-        gates = jnp.concatenate([gav[0], gav[1]], axis=0)
+        eye = (lax.broadcasted_iota(jnp.int32, (TOP, 128), 0) == lax.broadcasted_iota(jnp.int32, (TOP, 128), 1)).astype(F32)
+        ids = jnp.concatenate([turned(idv[n].astype(F32), eye) for n in range(2)], axis=0)
+        gates = jnp.concatenate([turned(gav[n], eye) for n in range(2)], axis=0)
         tri_i = lax.broadcasted_iota(jnp.int32, (2 * TOK, 2 * TOK), 0)
         tri_j = lax.broadcasted_iota(jnp.int32, (2 * TOK, 2 * TOK), 1)
         tri = jnp.where(jnp.logical_and(tri_j < tri_i, tri_i // TOK == tri_j // TOK), 1.0, 0.0).astype(BF16)
@@ -177,7 +187,7 @@
         for i in range(CHUNKS):
             lo, hi = groups_of(i)
             dz = jnp.where(col < HALF, lo * WINDOW, hi * WINDOW) + (col % HALF) // (2 * CAP)
-            wanted = 2 * lax.rem(z + NZ - dz, NZ) + c
+            wanted = (2 * lax.rem(z + NZ - dz, NZ) + c).astype(F32)
             hits = jnp.zeros((2 * TOK, ROWS), F32)
             share = jnp.zeros((2 * TOK, ROWS), F32)
             for k in range(TOP):
@@ -187,7 +197,8 @@
             rank = jnp.dot(tri, hits.astype(BF16), preferred_element_type=F32)
             table[i] = jnp.where(rank == slot, share, 0.0)
 
-    tok = WINDOW * PADTOK
+    part_tok = WINDOW * PADTOK
+    tok = 4 * part_tok
     lane = lax.broadcasted_iota(jnp.int32, (tok, 128), 1) - EDGE * (1 - odd)
     id_lane = jnp.logical_and(lane >= 0, lane < TOP)
     before_i = lax.broadcasted_iota(jnp.int32, (tok, tok), 0)
@@ -195,42 +206,44 @@
     before = jnp.where(
         jnp.logical_and(before_i < before_j, before_i // PADTOK == before_j // PADTOK), 1.0, 0.0
     ).astype(BF16)
-    slot_of = lax.broadcasted_iota(jnp.int32, (HALF, tok), 0)
-    tok_of = lax.broadcasted_iota(jnp.int32, (HALF, tok), 1)
-    ones = jnp.ones((HALF, 128), BF16)
-
-    def chosen(held, p):
+    tok_of = lax.broadcasted_iota(jnp.int32, (ROWS, tok), 1)
+    slot_of = lax.broadcasted_iota(jnp.int32, (ROWS, tok), 0)
+    first_slot = (
+        (tok_of // (2 * part_tok)) * HALF
+        + ((tok_of % part_tok) // PADTOK) * (2 * CAP)
+        + ((tok_of // part_tok) % 2) * CAP
+    )
+    wanted_rank = (slot_of - first_slot).astype(F32)
+    ones = jnp.ones((ROWS, 128), BF16)
+
+    def chosen(held):
         ids = jnp.where(odd == 1, held[:, :128].astype(F32), held[:, LANES - 128:].astype(F32))
         named = jnp.where(jnp.logical_and(id_lane, ids == e.astype(F32)), 1.0, 0.0).astype(BF16)
         hit = lax.dot_general(ones, named, (((1,), (1,)), ((), ())), preferred_element_type=F32)
         rank = jnp.dot(hit.astype(BF16), before, preferred_element_type=F32)
-        at = ((tok_of // PADTOK) * (2 * CAP) + p * CAP).astype(F32)
-        pick = jnp.where(rank + at == slot_of.astype(F32), hit, 0.0).astype(BF16)
+        pick = jnp.where(rank == wanted_rank, hit, 0.0).astype(BF16)
         return jnp.dot(pick, held, preferred_element_type=F32)
 
     def row_copy(i, d):
-        return remote(rows.at[y, i], rows.at[y, i], ysem.at[i, d], yrem.at[i, d], at_y(d))
+        return remote(rows.at[y, i], rows.at[y, i], ssem.at[2], yrem.at[i], at_y(d))
 
     def select(i):
-        for k in offsets_of(i):
-            over(k).wait_recv()
-        for n, g in enumerate(groups_of(i)):
-            own = ga[g * WINDOW:(g + 1) * WINDOW].reshape(tok, LANES)
-            other = gb[g * WINDOW:(g + 1) * WINDOW].reshape(tok, LANES)
-            picked = chosen(own, 0) + chosen(other, 1)
-            rows[y, i, n * HALF:(n + 1) * HALF, :] = jnp.where(own_lanes((HALF, LANES)), picked, 0.0).astype(BF16)
+        all_of(gb.at[pl.ds(0, 2 * WINDOW), pl.ds(0, TOK), :], brem.at[i])
+        held = jnp.concatenate(
+            [v[g * WINDOW:(g + 1) * WINDOW].reshape(part_tok, LANES) for g in groups_of(i) for v in (ga, gb)], axis=0
+        )
+        rows[y, i] = jnp.where(own_lanes((ROWS, LANES)), chosen(held), 0.0).astype(BF16)
         for d in (2, 1, 3):
             send(row_copy(i, d))
 
     def sum_copy(i, d):
-        return remote(gu.at[i, lax.rem(x + d, NX)], xin.at[i, d - 1], xsem.at[i, d], xrem.at[i, d], at_x(d))
+        return remote(gu.at[i, lax.rem(x + d, NX)], xin.at[i, d - 1], ssem.at[3], xrem.at[i], at_x(d))
 
     def multiply(i):
         if i == 0:
             loads[3].wait()
             loads[4].wait()
-        for d in (1, 3, 2):
-            row_copy(i, d).wait_recv()
+        all_of(yin.at[i], yrem.at[i])
         for n, w in ((0, wg), (1, wu)):
             total = jnp.dot(rows[0, i], w[:LANES, :], preferred_element_type=F32)
             for q in range(1, NY):
@@ -240,11 +253,10 @@
             send(sum_copy(i, d))
 
     def hid_copy(i, d):
-        return remote(hid.at[i, x], hid.at[i, x], hsem.at[i, d], hrem.at[i, d], at_x(d))
+        return remote(hid.at[i, x], hid.at[i, x], ssem.at[4], hrem.at[i], at_x(d))
 
     def activate(i):
-        for d in (1, 3, 2):
-            sum_copy(i, d).wait_recv()
+        all_of(xin.at[i], xrem.at[i])
         sums = (gu[i, x] + xin[i, 0]) + (xin[i, 1] + xin[i, 2])
         gate = sums[:, :256]
         up = sums[:, 256:]
@@ -253,25 +265,23 @@
             send(hid_copy(i, d))
 
     def down_copy(i, d):
-        return remote(down.at[i, lax.rem(y + d, NY)], yin.at[i, d - 1], dsem.at[i, d], drem.at[i, d], at_y(d))
+        return remote(down.at[i, lax.rem(y + d, NY)], yin.at[i, d - 1], ssem.at[5], drem.at[i], at_y(d))
 
     def project(i):
         if i == 0:
             loads[5].wait()
-        for d in (1, 3, 2):
-            hid_copy(i, d).wait_recv()
-        hidden = hid[i].reshape(ROWS, 256)
+        all_of(hid.at[i, pl.ds(0, NX - 1)], hrem.at[i])
+        hidden = hid[i].astype(F32).reshape(ROWS, 256).astype(BF16)
         for q in range(NY):
             down[i, q] = jnp.dot(hidden, wd[:, BASES[q]:BASES[q] + LANES], preferred_element_type=F32).astype(BF16)
         for d in (2, 1, 3):
             send(down_copy(i, d))
 
     def back_copy(k):
-        return remote(ret.at[k], back.at[k], zsem.at[k], zrem.at[k], at_z(k))
+        return remote(ret.at[k], back.at[k], ssem.at[6], zrem.at[chunk_of(k)], at_z(k))
 
     def give_back(i):
-        for d in (1, 3, 2):
-            down_copy(i, d).wait_recv()
+        all_of(yin.at[i], drem.at[i])
         result = (down[i, y].astype(F32) + yin[i, 0].astype(F32)) + (yin[i, 1].astype(F32) + yin[i, 2].astype(F32))
         result = result.reshape(2, WINDOW, 2 * CAP, LANES).astype(BF16)
         for n, g in enumerate(groups_of(i)):
@@ -283,9 +293,7 @@
                 send(back_copy(k))
 
     def mix(i):
-        for k in offsets_of(i):
-            if k != 0:
-                back_copy(k).wait_recv()
+        all_of(back.at[pl.ds(0, 2 * WINDOW - (i == 0))], zrem.at[i])
         arrived = jnp.concatenate(
             [back[g * WINDOW:(g + 1) * WINDOW].astype(F32).reshape(HALF, LANES) for g in groups_of(i)], axis=0
         )
@@ -301,6 +309,20 @@
         )):
             events.append((at, 100 - n, stage, i))
             at += STEP[wait]
+    def settle(n):
+        for copy in metas:
+            copy.wait_send()
+        all_of(ga.at[pl.ds(0, NZ - 1), pl.ds(0, TOK), :], ssem.at[0])
+        all_of(gb.at[:, pl.ds(0, TOK), :], ssem.at[1])
+        all_of(yin, ssem.at[2])
+        all_of(xin, ssem.at[3])
+        all_of(hid.at[:, pl.ds(0, NX - 1)], ssem.at[4])
+        all_of(yin, ssem.at[5])
+        all_of(ret.at[pl.ds(0, NZ - 1)], ssem.at[6])
+
+    late = max(at for at, _, stage, _ in events if stage is give_back)
+    events = [v if v[2] is not mix else (max(v[0], late + 1.0), *v[1:]) for v in events]
+    events.append((late + 0.5, 0, settle, 0))
     for _, _, stage, i in sorted(events, key=lambda v: v[:2] + (v[3],)):
         stage(i)
 
@@ -308,23 +330,25 @@
     part_copy = remote(part.at[0], part.at[1], psem.at[0], psem.at[1], partner)
     send(part_copy)
     part_copy.wait_recv()
+
+    def fin_copy(d):
+        return remote(fin.at[y], fin.at[y], ssem.at[7], frem.at[0], at_y(d))
+
     fin[y] = (acc[:TOK, :] + part[1]).astype(BF16)
-
-    def fin_copy(d):
-        return remote(fin.at[y], fin.at[y], fsem.at[d], frem.at[d], at_y(d))
-
     for d in (2, 1, 3):
         send(fin_copy(d))
-    for d in (1, 3, 2):
-        fin_copy(d).wait_recv()
+    all_of(fin.at[pl.ds(0, NY - 1)], frem.at[0])
     left = lax.broadcasted_iota(jnp.int32, (TOK, 128), 1) < EDGE
     for n in range(2):
         a, b, o = fin[2 * n], fin[2 * n + 1], n * 896
-        out_ref[:, o:o + 384] = a[:, :384]
-        out_ref[:, o + 384:o + 512] = jnp.where(left, a[:, 384:].astype(F32), b[:, :128].astype(F32)).astype(BF16)
-        out_ref[:, o + 512:o + 896] = b[:, 128:]
-    for copy in sent:
-        copy.wait_send()
+        outv[:, o:o + 384] = a[:, :384]
+        outv[:, o + 384:o + 512] = jnp.where(left, a[:, 384:].astype(F32), b[:, :128].astype(F32)).astype(BF16)
+        outv[:, o + 512:o + 896] = b[:, 128:]
+    stored = pltpu.make_async_copy(outv, out_ref, lsem.at[0])
+    stored.start()
+    part_copy.wait_send()
+    all_of(fin.at[pl.ds(0, NY - 1)], ssem.at[7])
+    stored.wait()
 
 
 def per_device(tokens, expert_ids, gate_weights, w_gate, w_up, w_down):
@@ -334,14 +358,14 @@
         body,
         out_shape=jax.ShapeDtypeStruct((TOK, 1792), BF16),
         in_specs=[pl.BlockSpec(memory_space=pl.ANY)] * 6,
-        out_specs=pl.BlockSpec(memory_space=pltpu.VMEM),
+        out_specs=pl.BlockSpec(memory_space=pl.ANY),
         scratch_shapes=[
             vm((1792, 256), BF16),
             vm((1792, 256), BF16),
             vm((256, 1792), BF16),
             vm((TOK, LANES), BF16),
-            vm((2, TOK, TOP), jnp.int32),
-            vm((2, TOK, TOP), F32),
+            vm((2, TOP, TOK), jnp.int32),
+            vm((2, TOP, TOK), F32),
             vm((NZ, PADTOK, LANES), BF16),
             vm((NZ, PADTOK, LANES), BF16),
             vm((NY, CHUNKS, ROWS, LANES), BF16),
@@ -356,15 +380,15 @@
             vm((2 * TOK, LANES), F32),
             vm((2, TOK, LANES), F32),
             vm((NY, TOK, LANES), BF16),
-            dma((6,)), dma((2,)), dma((2,)),
-            dma((NZ,)), dma((NZ,)), dma((NZ,)), dma((NZ,)),
-            *[dma((CHUNKS, 4))] * 8,
-            dma((NZ,)), dma((NZ,)), dma((2,)), dma((4,)), dma((4,)),
+            vm((TOK, 1792), BF16),
+            dma((6,)), dma((2,)), dma((2,)), dma((8,)), dma((NZ,)),
+            *[dma((CHUNKS,))] * 6,
+            dma((2,)), dma((1,)),
         ],
         compiler_params=pltpu.CompilerParams(
             collective_id=0, has_side_effects=True, vmem_limit_bytes=60 * 1024 * 1024
         ),
-    )(tokens, expert_ids, gate_weights, w_gate.reshape(1792, 256), w_up.reshape(1792, 256), w_down.reshape(256, 1792))
+    )(tokens, expert_ids.T, gate_weights.T, w_gate.reshape(1792, 256), w_up.reshape(1792, 256), w_down.reshape(256, 1792))
     return out
 
 

time: 103 us -> 94.4 us (0.917)
  Pallas kernels: 99.2 us -> 92.7 us
  local copies, waits for them, and re-layouts: 3.57 us -> 1.53 us
    pallas_call x1, Pallas kernels: 99.2 us -> 92.7 us  [per_device(): pl.pallas_call(body, out_shape=jax.ShapeDtypeStruct((TOK, 1792), BF16), i...]
    unnamed x7 -> x1, local copies, waits for them, and re-layouts: 3.57 us -> 1.53 us
where the time goes in v3:
time: 94.4 us; the launch traced here: 94.2 us
  Pallas kernels  92.7 us (98%)
  local copies, waits for them, and re-layouts  1.53 us (2%)
    pallas_call x1, Pallas kernels, per_device(): pl.pallas_call(body, out_shape=jax.ShapeDtypeStruct((TOK, 1792), BF16), i...  92.7 us

profile of v3, /device:TPU:1, one launch (start us, length us, event | category | flops | bytes accessed | tf_op | source)
XLA Modules:
  0.0 94.2 jit_solution(18143146928300152387)
XLA Ops:
  0.0 92.7 %shard_map.64 = bf16[24,1792]{1,0:T(8,128)(2,1)} custom-call(bf16[24,1792]{1,0:T(8,128)(2,1)} %tok_ref.1, s32[8,24]{1,0:T(8,128)} %bitcast.8, f32[8,24]{1,0:T(8,128)} %bitcast.9, bf16[1792,256]{1,0:T(8,128)(2,1)} %bitcast.5, bf16[1792,256]{1,0:T(8,128)(2,1)} %bitcast.6, bf16[256,1792]{1,0:T(8,128)(2,1)} %bitcast.7), custom_call_target="tpu_custom_call" | custom-call | tf_op jit(solution)/shard_map/pallas_call | solution.py:357
  92.7 1.5 %copy.8 = bf16[24,1792]{1,0:T(8,128)(2,1)} copy(bf16[24,1792]{1,0:T(8,128)(2,1)} %shard_map.64) | data formatting | bytes 172032
